TPU v7x, 32 devices: a whole 2x2x4 slice. The times are simulated.
32 devices in a mesh: gz: 16 (over z, y, x), gy: 2 (over core).
Axes of the slice: x: 2, y: 2, z: 4, core: 2. Of those that a mesh axis runs over, the one named last changes fastest.
Arguments:
- snapshots: float32 [48, 64, 128, 256], P(None, 'gz', 'gy'), may hold values from -6 to 6
- energies: float32 [48], replicated, may hold values from 0.3 to 3
- plane_weight: float32 [64], P('gz'), may hold values from 1 to 10
Outputs:
- modes: float32 [16, 64, 128, 256], P(None, 'gz', 'gy')
- basis: float32 [48, 16], replicated
All inputs are finite; a program needn't handle non-finite values.
Results may differ from a plain program's by a relative error of at most 0.0003.
Values sent between devices are 32-bit elements; how exact they have to be, the bound alone decides.
A program may use at most 128 MiB of HBM per device.

v0:
```python
import jax
import jax.numpy as jnp
from jax import lax
from jax.sharding import PartitionSpec as P

MODES = 16
ITERS = 6


def padded_2(block, sides, width):
    for axis, dim in sides:
        count = lax.axis_size(axis)
        forward = [(i, i + 1) for i in range(count - 1)]
        forward.append((count - 1, 0))
        backward = [(target, source) for source, target in forward]
        low = lax.ppermute(
            lax.slice_in_dim(block, block.shape[dim] - width, None, axis=dim), axis, forward
        )
        high = lax.ppermute(lax.slice_in_dim(block, 0, width, axis=dim), axis, backward)
        block = jnp.concatenate([low, block, high], axis=dim)
    return block


def local(snapshots, energies, plane_weight):
    count, planes, rows, width = snapshots.shape
    total = planes * lax.axis_size("gz") * rows * lax.axis_size("gy") * width
    scaled = snapshots * energies[:, None, None, None]
    padded = padded_2(scaled, (("gz", 1),), 1)
    filtered = 0.25 * padded[:, :-2] + 0.5 * scaled + 0.25 * padded[:, 2:]
    flat = filtered.reshape(count, -1)
    weighted = (filtered * plane_weight[None, :, None, None]).reshape(count, -1)
    partial_value = jnp.dot(weighted, flat.T, precision=lax.Precision.HIGHEST) / total
    gram = lax.psum(partial_value, ("gz", "gy"))
    basis = jnp.eye(count, dtype=jnp.float32)[:, :MODES]
    for step in range(ITERS):
        image = jnp.dot(gram, basis, precision=lax.Precision.HIGHEST)
        factor = jnp.linalg.cholesky(jnp.dot(image.T, image, precision=lax.Precision.HIGHEST))
        basis = jax.scipy.linalg.solve_triangular(factor, image.T, lower=True).T
    raw = jnp.dot(basis.T, flat, precision=lax.Precision.HIGHEST).reshape(
        MODES, planes, rows, width
    )
    projected = jnp.dot(gram, basis, precision=lax.Precision.HIGHEST)
    norms = jnp.sum(basis * projected, axis=0)
    modes = raw / jnp.sqrt(norms)[:, None, None, None]
    return (modes, basis)


def solution(mesh):
    placed = (P(None, "gz", "gy", None), P(), P("gz"))
    return jax.shard_map(
        local,
        mesh=mesh,
        in_specs=placed,
        out_specs=(P(None, "gz", "gy", None), P()),
        check_vma=False,
    )
```

profile of v0, /device:TPU:0, one launch (start us, length us, event | category | flops | bytes accessed | tf_op | source)
XLA Modules:
  0.0 292.3 jit_solution(18266743144551200550)
XLA Ops:
  0.6 12.0 %broadcast_multiply_fusion.1 = f32[48,4,64,256]{3,2,1,0:T(8,128)} fusion(f32[48,4,64,256]{3,2,1,0:T(8,128)} %param.6, f32[48]{0:T(128)} %param.7), kind=kLoop, calls=%fused_computation.12 | loop fusion | flops 3145728 | bytes 25166016 | tf_op jit(solution)/shard_map/mul | solution.py:27
  12.7 3.7 %fusion.67 = (f32[48,1,64,256]{3,2,1,0:T(8,128)S(1)}, f32[48,1,64,256]{3,2,1,0:T(8,128)S(1)}) fusion(f32[48,4,64,256]{3,2,1,0:T(8,128)} %broadcast_multiply_fusion.1), kind=kLoop, calls=%fused_computation.84 | loop fusion | bytes 12582912 | tf_op jit(solution)/shard_map/slice | solution.py:17
  16.4 3.0 %collective-permute-start = (f32[48,1,64,256]{3,2,1,0:T(8,128)S(1)}, f32[48,1,64,256]{3,2,1,0:T(8,128)}, u32[]{:S(2)}, u32[]{:S(2)}) collective-permute-start(f32[48,1,64,256]{3,2,1,0:T(8,128)S(1)} %get-tuple-element.10), channel_id=1, source_target_pairs={{0,2},{2,4},{4,6},{6,8},{8,10},{10,12},{12,14},{14,16},{16,18},{18... | collective-permute-start | bytes 9437192 | tf_op jit(solution)/shard_map/ppermute | solution.py:16
  19.4 4.1 %collective-permute-start.1 = (f32[48,1,64,256]{3,2,1,0:T(8,128)S(1)}, f32[48,1,64,256]{3,2,1,0:T(8,128)}, u32[]{:S(2)}, u32[]{:S(2)}) collective-permute-start(f32[48,1,64,256]{3,2,1,0:T(8,128)S(1)} %get-tuple-element.11), channel_id=1, source_target_pairs={{2,0},{4,2},{6,4},{8,6},{10,8},{12,10},{14,12},{16,14},{18,16},{20... | collective-permute-start | bytes 9437192 | tf_op jit(solution)/shard_map/ppermute | solution.py:19
  23.5 130.7 %collective-permute-done = f32[48,1,64,256]{3,2,1,0:T(8,128)} collective-permute-done((f32[48,1,64,256]{3,2,1,0:T(8,128)S(1)}, f32[48,1,64,256]{3,2,1,0:T(8,128)}, u32[]{:S(2)}, u32[]{:S(2)}) %collective-permute-start) | collective-permute-done | bytes 3145760 | tf_op jit(solution)/shard_map/ppermute | solution.py:16
  154.2 2.1 collective-permute-done.1
  156.3 13.5 %broadcast_multiply_fusion = (f32[48,4,64,256]{3,2,1,0:T(8,128)}, f32[48,4,64,256]{3,2,1,0:T(8,128)}) fusion(f32[4]{0:T(128)S(1)} %copy-done.2, f32[48,1,64,256]{3,2,1,0:T(8,128)} %collective-permute-done.1, f32[48,4,64,256]{3,2,1,0:T(8,128)S(1)} %copy-done, f32[48,1,64,256]{3,2,1,0:T(8,128)} %collective-permute-done), kind=kLoop, calls=%fused_computation.11 | loop fusion | flops 25165824 | bytes 44040208 | tf_op jit(solution)/shard_map/mul | solution.py:31
  169.7 32.1 %fusion.16 = f32[48,48]{1,0:T(8,128)S(1)} fusion(f32[48,4,64,256]{3,2,1,0:T(8,128)} %get-tuple-element.9, f32[48,4,64,256]{3,2,1,0:T(8,128)} %get-tuple-element.8), kind=kOutput, calls=%fused_computation.15 | convolution fusion | flops 1811941632 | bytes 25175040 | tf_op jit(solution)/shard_map/dot_general | solution.py:32
  201.8 39.7 %psum.7 = f32[48,48]{1,0:T(8,128)S(1)} all-reduce(f32[48,48]{1,0:T(8,128)S(1)} %fusion.16), channel_id=1, replica_groups=mesh['gz'=16,'gy'=2] {'gz','gy'}, use_global_device_ids=true, to_apply=%region_0.0 | all-reduce | flops 2304 | bytes 18432 | tf_op jit(solution)/shard_map/psum | solution.py:33
  242.0 1.5 cholesky.104
  244.1 0.6 fusion.24
  244.8 1.2 custom-call.10
  246.6 1.5 cholesky.115
  249.4 1.2 custom-call.11
  251.2 1.5 cholesky.126
  254.0 1.2 custom-call.12
  255.8 1.5 cholesky.137
  258.7 1.2 custom-call.13
  260.5 1.5 cholesky.148
  263.3 1.2 custom-call.14
  265.1 1.5 cholesky.159
  267.9 1.2 custom-call.15
  269.6 18.2 %broadcast_divide_fusion = f32[16,4,64,256]{3,0,2,1:T(8,128)S(1)} fusion(f32[16]{0:T(128)S(1)} %sqrt.7, f32[4,64,256,48]{2,1,0,3:T(8,128)} %bitcast.120, f32[16,48]{1,0:T(8,128)S(1)} %fusion.31), kind=kOutput, calls=%fused_computation.13 | convolution fusion | flops 605028352 | bytes 16780352 | tf_op jit(solution)/shard_map/dot_general | solution.py:39
  287.8 4.4 %copy.23 = f32[16,4,64,256]{3,2,1,0:T(8,128)} copy(f32[16,4,64,256]{3,0,2,1:T(8,128)S(1)} %broadcast_divide_fusion) | data formatting | bytes 8388608
  (55 shorter events, 11.2 us)
Async XLA Ops:
  12.7 143.6 %copy-start = (f32[48,4,64,256]{3,2,1,0:T(8,128)S(1)}, f32[48,4,64,256]{3,2,1,0:T(8,128)}, u32[]{:S(2)}) copy-start(f32[48,4,64,256]{3,2,1,0:T(8,128)} %broadcast_multiply_fusion.1) | copy-start | bytes 37748740
  12.7 143.6 %copy-start.2 = (f32[4]{0:T(128)S(1)}, f32[4]{0:T(128)}, u32[]{:S(2)}) copy-start(f32[4]{0:T(128)} %param.8) | copy-start | bytes 52
  16.4 137.8 %collective-permute-start = (f32[48,1,64,256]{3,2,1,0:T(8,128)S(1)}, f32[48,1,64,256]{3,2,1,0:T(8,128)}, u32[]{:S(2)}, u32[]{:S(2)}) collective-permute-start(f32[48,1,64,256]{3,2,1,0:T(8,128)S(1)} %get-tuple-element.10), channel_id=1, source_target_pairs={{0,2},{2,4},{4,6},{6,8},{8,10},{10,12},{12,14},{14,16},{16,18},{18... | collective-permute-start | bytes 9437192 | tf_op jit(solution)/shard_map/ppermute | solution.py:16
  19.4 136.8 %collective-permute-start.1 = (f32[48,1,64,256]{3,2,1,0:T(8,128)S(1)}, f32[48,1,64,256]{3,2,1,0:T(8,128)}, u32[]{:S(2)}, u32[]{:S(2)}) collective-permute-start(f32[48,1,64,256]{3,2,1,0:T(8,128)S(1)} %get-tuple-element.11), channel_id=1, source_target_pairs={{2,0},{4,2},{6,4},{8,6},{10,8},{12,10},{14,12},{16,14},{18,16},{20... | collective-permute-start | bytes 9437192 | tf_op jit(solution)/shard_map/ppermute | solution.py:19
  269.3 22.9 %copy-start.1 = (f32[16,48]{1,0:T(8,128)}, f32[16,48]{1,0:T(8,128)S(1)}, u32[]{:S(2)}) copy-start(f32[16,48]{1,0:T(8,128)S(1)} %fusion.31) | copy-start | bytes 9220
where the time goes:
time: 293 us; the launch traced here: 292 us
  waiting for transfers between devices  133 us (45%)
  matrix products  53.6 us (18%)
  other arithmetic  49.7 us (17%)
  blocking collectives  39.7 us (14%)
  local copies, waits for them, and re-layouts  8.63 us (3%)
  starting transfers between devices  7.08 us (2%)
    ppermute x1, waiting for transfers between devices, padded_2(): lax.ppermute(lax.slice_in_dim(block, block.shape[dim] - width, None, axis...  131 us
    psum x1, blocking collectives, local(): gram = lax.psum(partial_value, ('gz', 'gy'))  39.7 us
    dot_general x1, matrix products, local(): jnp.dot(weighted, flat.T, precision=lax.Precision.HIGHEST) / total  32.1 us
    dot_general x1, matrix products, local(): jnp.dot(basis.T, flat, precision=lax.Precision.HIGHEST)  18.2 us
    mul x1, other arithmetic, local(): weighted = (filtered * plane_weight[None, :, None, None]).reshape(count, -1)  13.5 us
    another operation x18, other arithmetic, local(): jnp.linalg.cholesky(jnp.dot(image.T, image, precision=lax.Precision.HIGHE...  12.9 us
    mul x1, other arithmetic, local(): scaled = snapshots * energies[:, None, None, None]  12 us
    another operation x12, other arithmetic, local(): basis = jax.scipy.linalg.solve_triangular(factor, image.T, lower=True).T  11.3 us
  transfers between devices with their start and end apart: 2, of which 2 were waited for; matrix products, arithmetic and copies ran while one was open for 0% of the time, Pallas kernels for 0%

commit v1 on v0

--- a/solution.py
+++ b/solution.py
@@ -30,7 +30,7 @@
     flat = filtered.reshape(count, -1)
     weighted = (filtered * plane_weight[None, :, None, None]).reshape(count, -1)
     partial_value = jnp.dot(weighted, flat.T, precision=lax.Precision.HIGHEST) / total
-    gram = lax.psum(partial_value, ("gz", "gy"))
+    gram = lax.psum(lax.psum(partial_value, axis_name="gz"), axis_name="gy")
     basis = jnp.eye(count, dtype=jnp.float32)[:, :MODES]
     for step in range(ITERS):
         image = jnp.dot(gram, basis, precision=lax.Precision.HIGHEST)

time: 293 us -> 331 us (1.13)
  blocking collectives: 39.7 us -> 78.3 us
    psum x1 -> x2, blocking collectives: 39.7 us -> 78.3 us  [local(): gram = lax.psum(lax.psum(partial_value, axis_name='gz'), axis_name='gy')]
where the time goes in v1:
time: 331 us
  waiting for transfers between devices  133 us (40%)
  blocking collectives  78.3 us (24%)
  matrix products  53.4 us (16%)
  other arithmetic  49.7 us (15%)
  local copies, waits for them, and re-layouts  8.63 us (3%)
  starting transfers between devices  7.08 us (2%)
    ppermute x1, waiting for transfers between devices, padded_2(): lax.ppermute(lax.slice_in_dim(block, block.shape[dim] - width, None, axis...  131 us
    psum x2, blocking collectives, local(): gram = lax.psum(lax.psum(partial_value, axis_name='gz'), axis_name='gy')  78.3 us
    dot_general x1, matrix products, local(): jnp.dot(weighted, flat.T, precision=lax.Precision.HIGHEST) / total  32.1 us
    dot_general x1, matrix products, local(): jnp.dot(basis.T, flat, precision=lax.Precision.HIGHEST)  17.9 us
    mul x1, other arithmetic, local(): weighted = (filtered * plane_weight[None, :, None, None]).reshape(count, -1)  13.5 us
    another operation x18, other arithmetic, local(): jnp.linalg.cholesky(jnp.dot(image.T, image, precision=lax.Precision.HIGHE...  12.9 us
    mul x1, other arithmetic, local(): scaled = snapshots * energies[:, None, None, None]  12 us
    another operation x12, other arithmetic, local(): basis = jax.scipy.linalg.solve_triangular(factor, image.T, lower=True).T  11.3 us
  transfers between devices with their start and end apart: 2, of which 2 were waited for; matrix products, arithmetic and copies ran while one was open for 0% of the time, Pallas kernels for 0%

profile of v1, /device:TPU:0, one launch (start us, length us, event | category | flops | bytes accessed | tf_op | source)
XLA Modules:
  0.0 330.6 jit_solution(15590672196728312854)
XLA Ops:
  0.6 12.0 %broadcast_multiply_fusion.1 = f32[48,4,64,256]{3,2,1,0:T(8,128)} fusion(f32[48,4,64,256]{3,2,1,0:T(8,128)} %param.6, f32[48]{0:T(128)} %param.7), kind=kLoop, calls=%fused_computation.12 | loop fusion | flops 3145728 | bytes 25166016 | tf_op jit(solution)/shard_map/mul | solution.py:27
  12.7 3.7 %fusion.67 = (f32[48,1,64,256]{3,2,1,0:T(8,128)S(1)}, f32[48,1,64,256]{3,2,1,0:T(8,128)S(1)}) fusion(f32[48,4,64,256]{3,2,1,0:T(8,128)} %broadcast_multiply_fusion.1), kind=kLoop, calls=%fused_computation.84 | loop fusion | bytes 12582912 | tf_op jit(solution)/shard_map/slice | solution.py:17
  16.4 3.0 collective-permute-start
  19.4 4.1 %collective-permute-start.1 = (f32[48,1,64,256]{3,2,1,0:T(8,128)S(1)}, f32[48,1,64,256]{3,2,1,0:T(8,128)}, u32[]{:S(2)}, u32[]{:S(2)}) collective-permute-start(f32[48,1,64,256]{3,2,1,0:T(8,128)S(1)} %get-tuple-element.11), channel_id=1, source_target_pairs={{2,0},{4,2},{6,4},{8,6},{10,8},{12,10},{14,12},{16,14},{18,16},{20... | collective-permute-start | bytes 9437192 | tf_op jit(solution)/shard_map/ppermute | solution.py:19
  23.5 130.7 %collective-permute-done = f32[48,1,64,256]{3,2,1,0:T(8,128)} collective-permute-done((f32[48,1,64,256]{3,2,1,0:T(8,128)S(1)}, f32[48,1,64,256]{3,2,1,0:T(8,128)}, u32[]{:S(2)}, u32[]{:S(2)}) %collective-permute-start) | collective-permute-done | bytes 3145760 | tf_op jit(solution)/shard_map/ppermute | solution.py:16
  154.2 2.1 collective-permute-done.1
  156.3 13.5 %broadcast_multiply_fusion = (f32[48,4,64,256]{3,2,1,0:T(8,128)}, f32[48,4,64,256]{3,2,1,0:T(8,128)}) fusion(f32[4]{0:T(128)S(1)} %copy-done.2, f32[48,1,64,256]{3,2,1,0:T(8,128)} %collective-permute-done.1, f32[48,4,64,256]{3,2,1,0:T(8,128)S(1)} %copy-done, f32[48,1,64,256]{3,2,1,0:T(8,128)} %collective-permute-done), kind=kLoop, calls=%fused_computation.11 | loop fusion | flops 25165824 | bytes 44040208 | tf_op jit(solution)/shard_map/mul | solution.py:31
  169.7 32.1 %fusion.16 = f32[48,48]{1,0:T(8,128)S(1)} fusion(f32[48,4,64,256]{3,2,1,0:T(8,128)} %get-tuple-element.9, f32[48,4,64,256]{3,2,1,0:T(8,128)} %get-tuple-element.8), kind=kOutput, calls=%fused_computation.15 | convolution fusion | flops 1811941632 | bytes 25175040 | tf_op jit(solution)/shard_map/dot_general | solution.py:32
  201.8 74.9 %psum.14 = f32[48,48]{1,0:T(8,128)S(1)} all-reduce(f32[48,48]{1,0:T(8,128)S(1)} %fusion.16), channel_id=1, replica_groups=mesh['gz'=16,'gy'=2] {'gz'}, use_global_device_ids=true, to_apply=%region_0.0 | all-reduce | flops 2304 | bytes 18432 | tf_op jit(solution)/shard_map/psum | solution.py:33
  276.8 3.4 %psum.15 = f32[48,48]{1,0:T(8,128)S(1)} all-reduce(f32[48,48]{1,0:T(8,128)S(1)} %psum.14), channel_id=1, replica_groups=mesh['gz'=16,'gy'=2] {'gy'}, use_global_device_ids=true, to_apply=%region_1.0 | all-reduce | flops 2304 | bytes 18432 | tf_op jit(solution)/shard_map/psum | solution.py:33
  280.6 1.5 cholesky.104
  283.4 1.2 custom-call.10
  285.2 1.5 cholesky.115
  288.0 1.2 custom-call.11
  289.8 1.5 cholesky.126
  292.6 1.2 custom-call.12
  294.4 1.5 cholesky.137
  297.2 1.2 custom-call.13
  299.1 1.5 cholesky.148
  301.9 1.2 custom-call.14
  303.7 1.5 cholesky.159
  306.5 1.2 custom-call.15
  308.2 17.9 %broadcast_divide_fusion = f32[16,4,64,256]{3,0,2,1:T(8,128)S(1)} fusion(f32[16]{0:T(128)S(1)} %sqrt.7, f32[4,64,256,48]{2,1,0,3:T(8,128)} %bitcast.120, f32[16,48]{1,0:T(8,128)S(1)} %fusion.31), kind=kOutput, calls=%fused_computation.13 | convolution fusion | flops 605028352 | bytes 16780352 | tf_op jit(solution)/shard_map/dot_general | solution.py:39
  326.1 4.4 %copy.23 = f32[16,4,64,256]{3,2,1,0:T(8,128)} copy(f32[16,4,64,256]{3,0,2,1:T(8,128)S(1)} %broadcast_divide_fusion) | data formatting | bytes 8388608
  (56 shorter events, 11.8 us)
Async XLA Ops:
  12.7 143.6 %copy-start = (f32[48,4,64,256]{3,2,1,0:T(8,128)S(1)}, f32[48,4,64,256]{3,2,1,0:T(8,128)}, u32[]{:S(2)}) copy-start(f32[48,4,64,256]{3,2,1,0:T(8,128)} %broadcast_multiply_fusion.1) | copy-start | bytes 37748740
  12.7 143.6 %copy-start.2 = (f32[4]{0:T(128)S(1)}, f32[4]{0:T(128)}, u32[]{:S(2)}) copy-start(f32[4]{0:T(128)} %param.8) | copy-start | bytes 52
  16.4 137.8 %collective-permute-start = (f32[48,1,64,256]{3,2,1,0:T(8,128)S(1)}, f32[48,1,64,256]{3,2,1,0:T(8,128)}, u32[]{:S(2)}, u32[]{:S(2)}) collective-permute-start(f32[48,1,64,256]{3,2,1,0:T(8,128)S(1)} %get-tuple-element.10), channel_id=1, source_target_pairs={{0,2},{2,4},{4,6},{6,8},{8,10},{10,12},{12,14},{14,16},{16,18},{18... | collective-permute-start | bytes 9437192 | tf_op jit(solution)/shard_map/ppermute | solution.py:16
  19.4 136.8 %collective-permute-start.1 = (f32[48,1,64,256]{3,2,1,0:T(8,128)S(1)}, f32[48,1,64,256]{3,2,1,0:T(8,128)}, u32[]{:S(2)}, u32[]{:S(2)}) collective-permute-start(f32[48,1,64,256]{3,2,1,0:T(8,128)S(1)} %get-tuple-element.11), channel_id=1, source_target_pairs={{2,0},{4,2},{6,4},{8,6},{10,8},{12,10},{14,12},{16,14},{18,16},{20... | collective-permute-start | bytes 9437192 | tf_op jit(solution)/shard_map/ppermute | solution.py:19
  307.9 22.7 %copy-start.1 = (f32[16,48]{1,0:T(8,128)}, f32[16,48]{1,0:T(8,128)S(1)}, u32[]{:S(2)}) copy-start(f32[16,48]{1,0:T(8,128)S(1)} %fusion.31) | copy-start | bytes 9220
